TPU v7x, 128 devices: a whole 4x4x4 slice. The times are simulated.
128 devices in a mesh: gx: 4 (over z), gy: 4 (over y), gz: 8 (over x, core).
Axes of the slice: x: 4, y: 4, z: 4, core: 2. Of those that a mesh axis runs over, the one named last changes fastest.
Arguments:
- positions: float32 [3, 64, 64, 2048], P(None, 'gx', 'gy', 'gz'), may hold values from -6 to 6
- pair_node: int32 [4, 4, 8, 32, 256], P('gx', 'gy', 'gz'), may hold values from 0 to 255
- pair_line: int32 [4, 4, 8, 32], P('gx', 'gy', 'gz'), may hold values from 0 to 255
- pair_far: int32 [4, 4, 8, 32, 256], P('gx', 'gy', 'gz'), may hold values from 0 to 261, as said below
- far_line: int32 [4, 4, 8, 32], P('gx', 'gy', 'gz'), may hold values from 0 to 483, as said below
- pair_geom: float32 [4, 4, 8, 32, 4, 256], P('gx', 'gy', 'gz'), may hold values from -4 to 4
- live_blocks: int32 [4, 4, 8], P('gx', 'gy', 'gz'), may hold values from 8 to 32, as said below
Outputs:
- corrected: float32 [3, 64, 64, 2048], P(None, 'gx', 'gy', 'gz')
- sweep_history: float32 [2, 5], replicated
Inputs may be any that keep to these rules, and one draw needn't show every extreme that they name: `pair_far`: together with far_line: at most one of the three coordinates of node b lies outside the owner block's own nodes; node b lies inside the whole grid; in slots below 16 node b is one of the owner block's own nodes. `far_line`: together with pair_far, as stated there. `live_blocks`: some owner block has all 32 slots live.
All inputs are finite; a program needn't handle non-finite values.
Results may differ from a plain program's by a relative error of at most 0.0001.
Values sent between devices are 32-bit elements; how exact they have to be, the bound alone decides.
A program may use at most 64 MiB of HBM per device.

v0:
```python
import functools

import jax
import jax.numpy as jnp
from jax import lax
from jax.experimental import pallas as pl
from jax.experimental.pallas import tpu as pltpu
from jax.sharding import PartitionSpec as P

RIM = 3
SWEEPS = 5
RELAX = 0.9
AXES = ("gx", "gy", "gz")
MESH = pl.DeviceIdType.MESH
f32 = jnp.float32
bf16 = jnp.bfloat16


def split(x, parts):
    out = []
    for _ in range(parts - 1):
        hi = x.astype(bf16)
        out.append(hi)
        x = x - hi.astype(f32)
    out.append(x.astype(bf16))
    return out


def mm(a, b):
    return jnp.dot(a, b, preferred_element_type=f32)


def take_lanes(x, low, half):
    outs = []
    for h in range(0, low.shape[1], 128):
        idx = low[:, h : h + 128]
        got = jnp.take_along_axis(x[:, :128], idx, axis=1, mode="promise_in_bounds")
        for j in range(1, x.shape[1] // 128):
            more = jnp.take_along_axis(
                x[:, 128 * j : 128 * (j + 1)], idx, axis=1, mode="promise_in_bounds"
            )
            got = jnp.where(half[:, h : h + 128] == j, more, got)
        outs.append(got)
    return jnp.concatenate(outs, axis=1)


def kernel(
    sizes,
    blk,
    live_ref,
    node_ref,
    line_ref,
    farpos_ref,
    farline_ref,
    geom_ref,
    pos_hbm,
    acc_ref,
    hist_ref,
    pos_ref,
    req,
    cols,
    hot,
    two,
    amat,
    cinv,
    geo,
    low_ref,
    half_ref,
    gap,
    wcat,
    reqs,
    dsend,
    drecv,
    erecv,
    rrecv,
    pos_sem,
    qs_sem,
    qr_sem,
    ds_sem,
    dr_sem,
    es_sem,
    er_sem,
    rs_sem,
    rr_sem,
):
    nx, ny, nz = sizes
    bx, by, bz = blk
    devices = nx * ny * nz
    blocks, pairs = gap.shape
    outer = blocks // 2
    lines = bx * by
    me = [lax.axis_index(a) for a in AXES]
    mine = (me[0] * ny + me[1]) * nz + me[2]
    dirs = [(a, s) for a in (1, 0, 2) for s in (1, -1)]

    def neighbour(axis, sign):
        to = list(me)
        to[axis] = lax.rem(me[axis] + sign + sizes[axis], sizes[axis])
        return tuple(to)

    def exists(axis, sign):
        return (me[axis] + sign >= 0) & (me[axis] + sign < sizes[axis])

    def coords(k):
        to = lax.rem(mine + k, devices)
        return (to // (ny * nz), lax.rem(to // nz, ny), lax.rem(to, nz))

    pos_copy = pltpu.make_async_copy(pos_hbm, pos_ref, pos_sem)
    pos_copy.start()

    def column(ref):
        row = ref[0, 0].astype(f32)
        return jnp.transpose(jnp.broadcast_to(row, (pairs, blocks)))

    wide = pairs // 128
    planes = [geom_ref[0, 0, 0, outer:, c, :] for c in range(3)]
    planes.append(farpos_ref[0, 0, 0, outer:, :].astype(f32))
    for c in range(4):
        for h in range(wide):
            req[c * wide + h] = planes[c][:, 128 * h : 128 * (h + 1)]
    cols[1] = column(farline_ref)
    req[4 * wide] = cols[1, outer:, :128]
    cols[0] = column(line_ref)
    def ask(d, axis, sign):
        return pltpu.make_async_remote_copy(
            src_ref=req,
            dst_ref=reqs.at[d],
            send_sem=qs_sem.at[d],
            recv_sem=qr_sem.at[d],
            device_id=neighbour(axis, sign),
            device_id_type=MESH,
        )

    for d, (axis, sign) in enumerate(dirs):

        @pl.when(exists(axis, sign))
        def _():
            ask(d, axis, sign).start()

    for d, (axis, sign) in enumerate(dirs):

        @pl.when(jnp.logical_not(exists(axis, -sign)))
        def _():
            reqs[d] = jnp.zeros(req.shape, f32)

        @pl.when(jnp.logical_not(exists(axis, sign)))
        def _():
            for t in range(SWEEPS):
                drecv[t, d] = jnp.zeros((outer, pairs), f32)

    live = jnp.broadcast_to(live_ref[0], (blocks, pairs))
    live_rows = lax.broadcasted_iota(jnp.int32, (blocks, pairs), 0) < live
    lane_node = lax.broadcasted_iota(jnp.int32, (pairs, bz), 1).astype(f32)
    node_t = jnp.transpose(node_ref[0, 0, 0].astype(f32))
    for b in range(blocks):
        hot[pl.ds(b * pairs, pairs), :] = jnp.where(
            node_t[:, b : b + 1] == lane_node, 1.0, 0.0
        ).astype(bf16)
    row_line = line_ref[0, 0].astype(f32)
    two[...] = jnp.concatenate([row_line, row_line], axis=1)
    row_mod = lax.broadcasted_iota(jnp.int32, (blocks, blocks), 0)
    col_mod = lax.broadcasted_iota(jnp.int32, (blocks, blocks), 1)
    line_b = cols[0]
    same = line_b[:, :blocks] == row_line
    first_col = 1.0 - jnp.max(
        jnp.where(same & (col_mod < row_mod), 1.0, 0.0), axis=1, keepdims=True
    )

    def expand(stack, step):
        rows = stack.shape[0]
        which = lax.rem(lax.broadcasted_iota(jnp.int32, (rows, pairs), 0), step)
        return jnp.concatenate(
            [jnp.where(which == j, stack, 0.0).astype(bf16) for j in range(step)], axis=1
        )

    counts = []
    for g in range(blocks // 8):
        ones = jnp.where(live_rows[8 * g : 8 * g + 8], 1.0, 0.0)
        counts.append(mm(expand(ones, 8), hot[pl.ds(8 * g * pairs, 8 * pairs), :]))
    counts = jnp.concatenate(counts, axis=0).astype(bf16)

    def located(code, zpos, shift):
        e = jnp.floor((code + 0.5) / (by + 2 * RIM))
        f = code - e * (by + 2 * RIM)
        e = e - (RIM + shift[0] * bx)
        f = f - (RIM + shift[1] * by)
        z = zpos - (RIM + shift[2] * bz)
        ok_line = (e >= 0) & (e < bx) & (f >= 0) & (f < by)
        return jnp.where(ok_line, e * by + f, -1.0), z, ok_line & (z >= 0) & (z < bz)

    def setup(row, line, node, geom):
        n = line.shape[0]
        lane_line = lax.broadcasted_iota(jnp.int32, (n, lines), 1).astype(f32)
        a = jnp.where(line[:, : 2 * blocks] == two[...], 1.0, 0.0).astype(bf16)
        amat[pl.ds(row, n), :] = a
        cinv[pl.ds(row, n), :] = RELAX / (1.0 + mm(a[:, :blocks], counts))
        idx = node.astype(jnp.int32)
        low = lax.bitwise_and(idx, 127)
        half = lax.shift_right_logical(idx, 7)
        low_ref[pl.ds(row, n), :] = low
        half_ref[pl.ds(row, n), :] = half
        own = jnp.where(line == lane_line, 1.0, 0.0).astype(bf16)
        total = jnp.zeros((n, pairs), f32)
        for c in range(3):
            geo[c, pl.ds(row, n), :] = geom[c]
            vals = jnp.zeros((n, bz), f32)
            for part in split(pos_ref[c].reshape(lines, bz), 3):
                vals += mm(own, part)
            total += geom[c] * take_lanes(vals, low, half)
        return total

    def cat(parts):
        return jnp.concatenate(parts, axis=0)

    pos_copy.wait()
    for d, (axis, sign) in enumerate(dirs):

        @pl.when(exists(axis, -sign))
        def _():
            ask(d, axis, sign).wait_recv()

    asked = []
    for d, (axis, sign) in enumerate(dirs):
        shift = [0, 0, 0]
        shift[axis] = sign
        got = [
            jnp.concatenate([reqs[d, c * wide + h] for h in range(wide)], axis=1) for c in range(4)
        ]
        code = jnp.concatenate([reqs[d, 4 * wide]] * wide, axis=1)
        line, z, ok = located(code, got[3], shift)
        asked.append(
            [line, jnp.where(ok, z, 0.0)] + [jnp.where(ok, -got[c], 0.0) for c in range(3)]
        )
    asked = [cat([x[i] for x in asked]) for i in range(5)]
    base = asked[0].shape[0]
    rows = base + 2 * blocks

    def respond(t, total):
        for d, (axis, sign) in enumerate(dirs):
            dsend[t, d] = total[d * outer : (d + 1) * outer]
        for d, (axis, sign) in enumerate(dirs):

            @pl.when(exists(axis, -sign))
            def _():
                answer(t, d, axis, sign).start()

    def answer(t, d, axis, sign):
        return pltpu.make_async_remote_copy(
            src_ref=dsend.at[t, d],
            dst_ref=drecv.at[t, d],
            send_sem=ds_sem.at[t, d],
            recv_sem=dr_sem.at[t, d],
            device_id=neighbour(axis, -sign),
            device_id_type=MESH,
        )

    def received(t):
        for d, (axis, sign) in enumerate(dirs):

            @pl.when(exists(axis, sign))
            def _():
                answer(t, d, axis, sign).wait_recv()

        got = drecv[t, 0]
        for d in range(1, len(dirs)):
            got = got + drecv[t, d]
        return got

    respond(0, setup(0, asked[0], asked[1], asked[2:]))

    line, z, ok = located(cols[1], farpos_ref[0, 0, 0].astype(f32), (0, 0, 0))
    geom = [geom_ref[0, 0, 0, :, c, :] for c in range(4)]
    start = setup(
        base,
        cat([line_b, line]),
        cat([node_ref[0, 0, 0].astype(f32), jnp.where(ok, z, 0.0)]),
        [cat([geom[c], jnp.where(ok, -geom[c], 0.0)]) for c in range(3)],
    )
    start = start[:blocks] + start[blocks:] - geom[3]
    gap[0:outer, :] = start[:outer]
    gap[pl.ds(outer, outer), :] = start[outer:] + received(0)
    acc_ref[...] = jnp.zeros_like(acc_ref)

    def to_all(ref, send_sem, recv_sem):
        def send(k, carry):
            pltpu.make_async_remote_copy(
                src_ref=ref,
                dst_ref=ref,
                send_sem=send_sem,
                recv_sem=recv_sem,
                device_id=coords(k),
                device_id_type=MESH,
            ).start()
            return carry

        lax.fori_loop(1, devices, send, 0, unroll=devices <= 32)

    def lanes_sum(x):
        x = jnp.sum(x, axis=0, keepdims=True)
        out = x[:, :128]
        for j in range(1, x.shape[1] // 128):
            out = out + x[:, 128 * j : 128 * (j + 1)]
        return out

    lane = lax.broadcasted_iota(jnp.int32, (1, 128), 1)

    def apply(row, n, parts):
        both = mm(amat[row : row + n, :], parts)
        return [both[:, c * bz : (c + 1) * bz] * cinv[row : row + n, :] for c in range(3)]

    def dots(row, n, moved):
        low = low_ref[row : row + n, :]
        half = half_ref[row : row + n, :]
        total = geo[0, row : row + n] * take_lanes(moved[0], low, half)
        for c in range(1, 3):
            total += geo[c, row : row + n] * take_lanes(moved[c], low, half)
        return total

    def sweep(t, last):
        depth = jnp.where(live_rows, jnp.maximum(-gap[...], 0.0), 0.0)
        squares = lanes_sum(depth * depth)
        if not last:
            erecv[t, mine] = squares
            to_all(erecv.at[t, mine], es_sem.at[t], er_sem.at[t])
        for g in range(blocks // 8):
            lo, hi = 8 * g, 8 * g + 8
            terms = cat([depth[lo:hi] * geo[c, base + lo : base + hi] for c in range(3)])
            top = terms.astype(bf16).astype(f32)
            sums = mm(expand(cat([top, terms - top]), 8), hot[pl.ds(lo * pairs, 8 * pairs), :])
            sums = sums[:24] + sums[24:]
            for c in range(3):
                wcat[lo:hi, c * bz : (c + 1) * bz] = sums[8 * c : 8 * c + 8]
        parts = cat(split(wcat[...], 2))
        if not last:
            respond(t + 1, dots(0, base, apply(0, base, parts)))
        moved = apply(base, blocks if last else 2 * blocks, parts)
        near = jnp.concatenate([m[:blocks] for m in moved], axis=1)
        resid = jnp.sum(lanes_sum(near * near * first_col), axis=1, keepdims=True)
        rrecv[mine] = jnp.where(lane == t, resid, rrecv[mine])
        if last:
            energy = jnp.sum(squares, axis=1, keepdims=True)
            rrecv[mine] = jnp.where(lane == SWEEPS, energy, rrecv[mine])
            to_all(rrecv.at[mine], rs_sem, rr_sem)
            others = rrecv.at[pl.ds(0, devices - 1)]
            pltpu.make_async_copy(others, others, rr_sem).wait()
            energy = jnp.sum(rrecv[...], axis=0)[:, SWEEPS : SWEEPS + 1]
        else:
            step = dots(base, 2 * blocks, moved)
            step = step[:blocks] + step[blocks:]
            others = erecv.at[t, pl.ds(0, devices - 1)]
            pltpu.make_async_copy(others, others, er_sem.at[t]).wait()
            energy = jnp.sum(jnp.sum(erecv[t], axis=0), axis=1, keepdims=True)
        scale = 1.0 / (1.0 + energy / (blocks * pairs * devices))
        hist_ref[0:1, :] = jnp.where(lane == t, energy, hist_ref[0:1, :])
        hist_ref[1:2, :] = jnp.where(lane == t, scale, hist_ref[1:2, :])
        acc_ref[...] = acc_ref[...] + (scale * first_col) * near
        if not last:
            more = received(t + 1)
            gap[0:outer, :] = gap[0:outer, :] + scale * step[:outer]
            gap[pl.ds(outer, outer), :] = gap[pl.ds(outer, outer), :] + scale * (
                step[outer:] + more
            )

    rrecv[mine] = jnp.zeros((1, 128), f32)
    hist_ref[...] = jnp.zeros_like(hist_ref)

    def body(t, carry):
        sweep(t, False)
        return carry

    lax.fori_loop(0, SWEEPS - 1, body, 0)
    sweep(SWEEPS - 1, True)

    for d, (axis, sign) in enumerate(dirs):

        @pl.when(exists(axis, sign))
        def _():
            ask(d, axis, sign).wait_send()

        @pl.when(exists(axis, -sign))
        def _():
            for t in range(SWEEPS):
                answer(t, d, axis, sign).wait_send()

    for t in range(SWEEPS - 1):
        ref = erecv.at[t, pl.ds(0, devices - 1)]
        pltpu.make_async_copy(ref, ref, es_sem.at[t]).wait()
    others = rrecv.at[pl.ds(0, devices - 1)]
    pltpu.make_async_copy(others, others, rs_sem).wait()
    energy, scale = hist_ref[0:1, :], hist_ref[1:2, :]
    resid = jnp.sum(rrecv[...], axis=0)
    hist_ref[0:1, :] = jnp.sqrt(1.0 + energy / (blocks * pairs))
    hist_ref[1:2, :] = jnp.sqrt(1.0 + scale * scale * resid / (bx * by * bz))


def finish(acc_ref, line_ref, hist_in, pos_ref, out_ref, hist_ref):
    _, bx, by, bz = pos_ref.shape
    lines = bx * by
    row = line_ref[0, 0].astype(f32)
    row = jnp.concatenate([row, row], axis=1)
    rows = lax.broadcasted_iota(jnp.int32, (lines, row.shape[1]), 0).astype(f32)
    place = jnp.where(rows == row, 1.0, 0.0).astype(bf16)
    total = mm(place, jnp.concatenate(split(acc_ref[...], 2), axis=0))
    out_ref[0] = pos_ref[0] + total.reshape(bx, by, bz)
    hist_ref[...] = hist_in[0:2, : hist_ref.shape[1]]


def local(sizes, positions, pair_node, pair_line, pair_far, far_line, pair_geom, live_blocks):
    blocks, pairs = pair_node.shape[3:]
    blk = positions.shape[1:]
    devices = sizes[0] * sizes[1] * sizes[2]
    outer = blocks // 2
    rows = 2 * blocks + 6 * outer
    dma = pltpu.SemaphoreType.DMA
    vmem = pl.BlockSpec(memory_space=pltpu.VMEM)
    moved, hist = pl.pallas_call(
        functools.partial(kernel, sizes, blk),
        out_shape=(
            jax.ShapeDtypeStruct((blocks, 3 * blk[2]), f32),
            jax.ShapeDtypeStruct((8, 128), f32),
        ),
        in_specs=[vmem] * 6 + [pl.BlockSpec(memory_space=pl.ANY)],
        out_specs=(vmem, vmem),
        scratch_shapes=[
            pltpu.VMEM(positions.shape, f32),
            pltpu.VMEM((4 * (pairs // 128) + 1, outer, 128), f32),
            pltpu.VMEM((2, blocks, pairs), f32),
            pltpu.VMEM((blocks * pairs, blk[2]), bf16),
            pltpu.VMEM((1, 2 * blocks), f32),
            pltpu.VMEM((rows, 2 * blocks), bf16),
            pltpu.VMEM((rows, pairs), f32),
            pltpu.VMEM((3, rows, pairs), f32),
            pltpu.VMEM((rows, pairs), jnp.int32),
            pltpu.VMEM((rows, pairs), jnp.int32),
            pltpu.VMEM((blocks, pairs), f32),
            pltpu.VMEM((blocks, 3 * blk[2]), f32),
            pltpu.VMEM((6, 4 * (pairs // 128) + 1, outer, 128), f32),
            pltpu.VMEM((SWEEPS, 6, outer, pairs), f32),
            pltpu.VMEM((SWEEPS, 6, outer, pairs), f32),
            pltpu.VMEM((SWEEPS, devices, 1, 128), f32),
            pltpu.VMEM((devices, 1, 128), f32),
            dma,
            dma((6,)),
            dma((6,)),
            dma((SWEEPS, 6)),
            dma((SWEEPS, 6)),
            dma((SWEEPS,)),
            dma((SWEEPS,)),
            dma,
            dma,
        ],
        compiler_params=pltpu.CompilerParams(has_side_effects=True),
    )(live_blocks, pair_node, pair_line, pair_far, far_line, pair_geom, positions)
    return pl.pallas_call(
        finish,
        grid=(3,),
        out_shape=(
            jax.ShapeDtypeStruct(positions.shape, f32),
            jax.ShapeDtypeStruct((2, SWEEPS), f32),
        ),
        in_specs=[
            pl.BlockSpec((blocks, blk[2]), lambda c: (0, c)),
            pl.BlockSpec(pair_line.shape, lambda c: (0, 0, 0, 0)),
            pl.BlockSpec((8, 128), lambda c: (0, 0)),
            pl.BlockSpec((1,) + blk, lambda c: (c, 0, 0, 0)),
        ],
        out_specs=(
            pl.BlockSpec((1,) + blk, lambda c: (c, 0, 0, 0)),
            pl.BlockSpec((2, SWEEPS), lambda c: (0, 0)),
        ),
    )(moved, pair_line, hist, positions)


def solution(mesh):
    sizes = tuple(mesh.shape[a] for a in AXES)
    return jax.shard_map(
        functools.partial(local, sizes),
        mesh=mesh,
        in_specs=(
            P(None, "gx", "gy", "gz"),
            P("gx", "gy", "gz", None, None),
            P("gx", "gy", "gz", None),
            P("gx", "gy", "gz", None, None),
            P("gx", "gy", "gz", None),
            P("gx", "gy", "gz", None, None, None),
            P("gx", "gy", "gz"),
        ),
        out_specs=(P(None, "gx", "gy", "gz"), P()),
        check_vma=False,
    )
```

profile of v0, /device:TPU:1, one launch (start us, length us, event | category | flops | bytes accessed | tf_op | source)
XLA Modules:
  0.0 69.2 jit_solution(13158591558293214413)
XLA Ops:
  1.3 64.7 %shard_map.86 = (f32[32,768]{1,0:T(8,128)}, f32[8,128]{1,0:T(8,128)}) custom-call(s32[1,1,1]{2,1,0:T(1,128)S(6)} %copy.9.live_ref, s32[1,1,1,32,256]{4,3,2,1,0:T(8,128)} %node_ref.1, s32[1,1,1,32]{3,2,1,0:T(1,128)} %line_ref.3, s32[1,1,1,32,256]{4,3,2,1,0:T(8,128)} %farpos_ref.1, s32[1,1,1,32]{3,2,1,0:T(1,128)} %farline_ref.1, ...), custom_call_target="tpu_custom_call" | custom-call | tf_op jit(solution)/shard_map/pallas_call | solution.py:416
  65.9 3.2 %shard_map.87 = (f32[3,16,16,256]{3,2,1,0:T(8,128)}, f32[2,5]{1,0:T(2,128)}) custom-call(f32[32,768]{1,0:T(8,128)} %get-tuple-element.4.acc_ref, s32[1,1,1,32]{3,2,1,0:T(1,128)} %line_ref.3, f32[8,128]{1,0:T(8,128)} %get-tuple-element.5.hist_in, f32[3,16,16,256]{3,2,1,0:T(8,128)} %pos_ref.1), custom_call_target="tpu_custom_call" | custom-call | tf_op jit(solution)/shard_map/pallas_call | solution.py:454
where the time goes:
time: 69.4 us; the launch traced here: 69.2 us
  Pallas kernels  67.9 us (98%)
  between operations  1.29 us (2%)
    pallas_call x1, Pallas kernels, local(): pl.pallas_call(functools.partial(kernel, sizes, blk), out_shape=(jax.Shap...  64.7 us
    pallas_call x1, Pallas kernels, local(): pl.pallas_call(finish, grid=(3,), out_shape=(jax.ShapeDtypeStruct(positio...  3.24 us

commit v1 on v0

v1 whole, which is shorter than its diff:
```python
import functools
import itertools

import jax
import jax.numpy as jnp
from jax import lax
from jax.experimental import pallas as pl
from jax.experimental.pallas import tpu as pltpu
from jax.sharding import PartitionSpec as P

RIM = 3
SWEEPS = 5
RELAX = 0.9
AXES = ("gx", "gy", "gz")
MESH = pl.DeviceIdType.MESH
f32 = jnp.float32
bf16 = jnp.bfloat16
i32 = jnp.int32
DIRS = [(a, s) for a in (1, 0, 2) for s in (1, -1)]


def scope(name):
    return jax.named_scope(name)


def split(x, parts):
    out = []
    for _ in range(parts - 1):
        hi = x.astype(bf16)
        out.append(hi)
        x = x - hi.astype(f32)
    out.append(x.astype(bf16))
    return out


def mm(a, b):
    return jnp.dot(a, b, preferred_element_type=f32)


def cat(parts):
    return jnp.concatenate(parts, axis=0)


def take_lanes(x, low, half):
    outs = []
    for h in range(0, low.shape[1], 128):
        idx = low[:, h : h + 128]
        got = jnp.take_along_axis(x[:, :128], idx, axis=1, mode="promise_in_bounds")
        for j in range(1, x.shape[1] // 128):
            more = jnp.take_along_axis(
                x[:, 128 * j : 128 * (j + 1)], idx, axis=1, mode="promise_in_bounds"
            )
            got = jnp.where(half[:, h : h + 128] == j, more, got)
        outs.append(got)
    return jnp.concatenate(outs, axis=1)


def kernel(
    sizes,
    blk,
    live_hbm,
    node_hbm,
    line_hbm,
    far_hbm,
    farline_hbm,
    geom_hbm,
    pos_hbm,
    out_ref,
    hist_ref,
    pos_v,
    node_v,
    far_v,
    geom_v,
    line_v,
    farline_v,
    live_v,
    rfar,
    rline,
    rgeom,
    ppart,
    hot,
    amat,
    geo,
    low_ref,
    half_ref,
    cinv,
    gap,
    wcat,
    acc,
    track,
    vsend,
    vrecv,
    dsend,
    drecv,
    erecv,
    rrecv,
    in_sem,
    qs_sem,
    qr_sem,
    vs_sem,
    vr_sem,
    ds_sem,
    dr_sem,
    es_sem,
    er_sem,
    rs_sem,
    rr_sem,
    plane_sem,
    all_sem,
):
    nx, ny, nz = sizes
    bx, by, bz = blk
    devices = nx * ny * nz
    blocks, pairs = gap.shape
    outer = blocks // 2
    lines = bx * by
    base = len(DIRS) * outer
    me = [lax.axis_index(a) for a in AXES]
    mine = (me[0] * ny + me[1]) * nz + me[2]

    def at_offset(off):
        return tuple(lax.rem(me[a] + off[a], sizes[a]) if off[a] else me[a] for a in range(3))

    def neighbour(axis, sign):
        off = [0, 0, 0]
        off[axis] = sign % sizes[axis]
        return at_offset(off)

    def exists(axis, sign):
        return (me[axis] + sign >= 0) & (me[axis] + sign < sizes[axis])

    def along(axis):
        return [tuple(o if a == axis else 0 for a in range(3)) for o in range(1, sizes[axis])]

    with scope("entry"):
        barrier = pltpu.get_barrier_semaphore()
        close = along(2) + along(1) + along(0)
        for off in close:
            pl.semaphore_signal(barrier, inc=1, device_id=at_offset(off), device_id_type=MESH)
        loads = [
            pltpu.make_async_copy(src, dst, in_sem.at[i])
            for i, (src, dst) in enumerate(
                [
                    (far_hbm.at[0, 0, 0], far_v),
                    (farline_hbm.at[0, 0], farline_v),
                    (geom_hbm.at[0, 0, 0], geom_v),
                    (pos_hbm, pos_v),
                    (node_hbm.at[0, 0, 0], node_v),
                    (line_hbm.at[0, 0], line_v),
                    (live_hbm.at[0], live_v),
                ]
            )
        ]
        for load in loads:
            load.start()
        loads[0].wait()
        loads[1].wait()
        pl.semaphore_wait(barrier, len(close))

    asks = [
        (far_v.at[pl.ds(outer, outer)], rfar),
        (farline_v, rline),
        (geom_v.at[pl.ds(outer, outer)], rgeom),
    ]

    def ask(i, d, axis, sign):
        return pltpu.make_async_remote_copy(
            src_ref=asks[i][0],
            dst_ref=asks[i][1].at[d],
            send_sem=qs_sem.at[i, d],
            recv_sem=qr_sem.at[i, d],
            device_id=neighbour(axis, sign),
            device_id_type=MESH,
        )

    with scope("ask"):
        for d, (axis, sign) in enumerate(DIRS):

            @pl.when(exists(axis, sign))
            def _():
                ask(1, d, axis, sign).start()
                ask(0, d, axis, sign).start()

        for off in along(1):
            pl.semaphore_signal(plane_sem, inc=1, device_id=at_offset(off), device_id_type=MESH)
        loads[2].wait()
        for d, (axis, sign) in enumerate(DIRS):

            @pl.when(exists(axis, sign))
            def _():
                ask(2, d, axis, sign).start()

            @pl.when(jnp.logical_not(exists(axis, -sign)))
            def _():
                rfar[d] = jnp.zeros((outer, pairs), i32)
                rline[d] = jnp.zeros((1, blocks), i32)
                rgeom[d] = jnp.zeros((outer, 4, pairs), f32)

            @pl.when(jnp.logical_not(exists(axis, sign)))
            def _():
                vrecv[d] = jnp.zeros((3, outer, pairs), f32)
                for t in range(SWEEPS - 1):
                    drecv[t, d] = jnp.zeros((outer, pairs), f32)

    with scope("parts"):
        loads[3].wait()
        for c in range(3):
            for i, part in enumerate(split(pos_v[c].reshape(lines, bz), 3)):
                ppart[c, i] = part

    with scope("hot"):
        for load in loads[4:]:
            load.wait()
        lane_node = lax.broadcasted_iota(i32, (pairs, bz), 1).astype(f32)
        node_t = jnp.transpose(node_v[...].astype(f32))
        for b in range(blocks):
            hot[pl.ds(b * pairs, pairs), :] = jnp.where(
                node_t[:, b : b + 1] == lane_node, 1.0, 0.0
            ).astype(bf16)

    row_line = line_v[...].astype(f32)
    two = jnp.concatenate([row_line, row_line], axis=1)
    lane_line = lax.broadcasted_iota(i32, (1, lines), 1).astype(f32)

    def column(row, first, n):
        r = lax.broadcasted_iota(i32, (n, blocks), 0)
        l = lax.broadcasted_iota(i32, (n, blocks), 1)
        return jnp.sum(jnp.where(l == r + first, row, 0.0), axis=1, keepdims=True)

    def located(code, zpos, shift):
        e = jnp.floor((code + 0.5) / (by + 2 * RIM))
        f = code - e * (by + 2 * RIM)
        e = e - (RIM + shift[0] * bx)
        f = f - (RIM + shift[1] * by)
        z = zpos - (RIM + shift[2] * bz)
        ok_line = (e >= 0) & (e < bx) & (f >= 0) & (f < by)
        ok = ok_line & (z >= 0) & (z < bz)
        return jnp.where(ok_line, e * by + f, -1.0), jnp.where(ok, z, 0.0), ok

    def place(row, line, node):
        n = line.shape[0]
        amat[pl.ds(row, n), :] = jnp.where(line == two, 1.0, 0.0).astype(bf16)
        idx = node.astype(i32)
        low = lax.bitwise_and(idx, 127)
        half = lax.shift_right_logical(idx, 7)
        low_ref[pl.ds(row, n), :] = low
        half_ref[pl.ds(row, n), :] = half
        own = jnp.where(line == lane_line, 1.0, 0.0).astype(bf16)
        out = []
        for c in range(3):
            vals = mm(own, ppart[c, 0]) + mm(own, ppart[c, 1]) + mm(own, ppart[c, 2])
            out.append(take_lanes(vals, low, half))
        return out

    with scope("known"):
        pl.semaphore_wait(plane_sem, ny - 1)
        for off in along(2):
            pl.semaphore_signal(all_sem, inc=1, device_id=at_offset(off), device_id_type=MESH)

    with scope("ask_wait"):
        for d, (axis, sign) in enumerate(DIRS):

            @pl.when(exists(axis, -sign))
            def _():
                ask(1, d, axis, sign).wait_recv()
                ask(0, d, axis, sign).wait_recv()

    def give(d, axis, sign):
        return pltpu.make_async_remote_copy(
            src_ref=vsend.at[d],
            dst_ref=vrecv.at[d],
            send_sem=vs_sem.at[d],
            recv_sem=vr_sem.at[d],
            device_id=neighbour(axis, -sign),
            device_id_type=MESH,
        )

    with scope("give"):
        asked_line, asked_node, asked_ok = [], [], []
        for d, (axis, sign) in enumerate(DIRS):
            shift = [0, 0, 0]
            shift[axis] = sign
            code = column(rline[d].astype(f32), outer, outer)
            line, z, ok = located(code, rfar[d].astype(f32), shift)
            asked_line.append(line)
            asked_node.append(z)
            asked_ok.append(jnp.where(ok, 1.0, 0.0))
        asked_ok = cat(asked_ok)
        vals = place(0, cat(asked_line), cat(asked_node))
        for c in range(3):
            got = vals[c] * asked_ok
            for d in range(len(DIRS)):
                vsend[d, c] = got[d * outer : (d + 1) * outer]
        for d, (axis, sign) in enumerate(DIRS):

            @pl.when(exists(axis, -sign))
            def _():
                give(d, axis, sign).start()

    with scope("counts"):
        live = jnp.broadcast_to(live_v[...], (blocks, pairs))
        live_rows = lax.broadcasted_iota(i32, (blocks, pairs), 0) < live

        def expand(stack, step):
            rows = stack.shape[0]
            which = lax.rem(lax.broadcasted_iota(i32, (rows, pairs), 0), step)
            return jnp.concatenate(
                [jnp.where(which == j, stack, 0.0).astype(bf16) for j in range(step)], axis=1
            )

        counts = []
        for g in range(blocks // 8):
            ones = jnp.where(live_rows[8 * g : 8 * g + 8], 1.0, 0.0)
            counts.append(mm(expand(ones, 8), hot[pl.ds(8 * g * pairs, 8 * pairs), :]))
        counts = cat(counts).astype(bf16)
        line_col = column(row_line, 0, blocks)
        same = line_col == row_line
        row_mod = lax.broadcasted_iota(i32, (blocks, blocks), 0)
        col_mod = lax.broadcasted_iota(i32, (blocks, blocks), 1)
        first_col = 1.0 - jnp.max(
            jnp.where(same & (col_mod < row_mod), 1.0, 0.0), axis=1, keepdims=True
        )
        cinv[...] = RELAX / (1.0 + mm(jnp.where(same, 1.0, 0.0).astype(bf16), counts))

    with scope("own"):
        code = column(farline_v[...].astype(f32), 0, blocks)
        line, z, ok = located(code, far_v[...].astype(f32), (0, 0, 0))
        here = jnp.where(ok, 1.0, 0.0)
        vals = place(base, cat([line_col, line]), cat([node_v[...].astype(f32), z]))
        start = -geom_v[:, 3, :]
        for c in range(3):
            g = geom_v[:, c, :]
            away = -(g * here)
            geo[c, pl.ds(base, blocks), :] = g
            geo[c, pl.ds(base + blocks, blocks), :] = away
            start += g * vals[c][:blocks] + away * vals[c][blocks:]
        gap[...] = start
        acc[...] = jnp.zeros_like(acc)
        track[...] = jnp.zeros_like(track)
        rrecv[mine] = jnp.zeros((1, 128), f32)

    with scope("geo"):
        for d, (axis, sign) in enumerate(DIRS):

            @pl.when(exists(axis, -sign))
            def _():
                ask(2, d, axis, sign).wait_recv()

        for d in range(len(DIRS)):
            for c in range(3):
                rows = slice(d * outer, (d + 1) * outer)
                geo[c, rows, :] = -(rgeom[d, :, c, :] * asked_ok[rows])

    with scope("give_wait"):
        pl.semaphore_wait(all_sem, nz - 1)
        for d, (axis, sign) in enumerate(DIRS):

            @pl.when(exists(axis, sign))
            def _():
                give(d, axis, sign).wait_recv()

        more = jnp.zeros((outer, pairs), f32)
        for c in range(3):
            far = vrecv[0, c]
            for d in range(1, len(DIRS)):
                far = far + vrecv[d, c]
            more = more + geom_v[outer:, c, :] * far
        gap[pl.ds(outer, outer), :] = gap[pl.ds(outer, outer), :] - more

    def answer(t, d, axis, sign):
        return pltpu.make_async_remote_copy(
            src_ref=dsend.at[t, d],
            dst_ref=drecv.at[t, d],
            send_sem=ds_sem.at[t, d],
            recv_sem=dr_sem.at[t, d],
            device_id=neighbour(axis, -sign),
            device_id_type=MESH,
        )

    def hops(off):
        x, core = off[2] // 2, off[2] % 2
        far = [min(o, s - o) for o, s in ((off[0], nx), (off[1], ny), (x, nz // 2))]
        return sum(far) + 0.3 * core

    everyone = sorted(
        (o for o in itertools.product(range(nx), range(ny), range(nz)) if any(o)),
        key=hops,
        reverse=True,
    )

    def to_all(ref, send_sem, recv_sem):
        for off in everyone:
            pltpu.make_async_remote_copy(
                src_ref=ref,
                dst_ref=ref,
                send_sem=send_sem,
                recv_sem=recv_sem,
                device_id=at_offset(off),
                device_id_type=MESH,
            ).start()

    def lanes_sum(x):
        x = jnp.sum(x, axis=0, keepdims=True)
        out = x[:, :128]
        for j in range(1, x.shape[1] // 128):
            out = out + x[:, 128 * j : 128 * (j + 1)]
        return out

    lane = lax.broadcasted_iota(i32, (1, 128), 1)

    def dots(row, n, moved):
        low = low_ref[row : row + n, :]
        half = half_ref[row : row + n, :]
        total = geo[0, row : row + n] * take_lanes(moved[:, :bz], low, half)
        for c in range(1, 3):
            total += geo[c, row : row + n] * take_lanes(
                moved[:, c * bz : (c + 1) * bz], low, half
            )
        return total

    def sweep(t, last):
        with scope("energy"):
            depth = jnp.where(live_rows, jnp.maximum(-gap[...], 0.0), 0.0)
            squares = lanes_sum(depth * depth)
            if not last:
                erecv[t, mine] = squares
                to_all(erecv.at[t, mine], es_sem.at[t], er_sem.at[t])
        with scope("scatter"):
            for g in range(blocks // 8):
                lo, hi = 8 * g, 8 * g + 8
                terms = cat(
                    [depth[lo:hi] * geo[c, base + lo : base + hi] for c in range(3)]
                )
                top = terms.astype(bf16).astype(f32)
                sums = mm(
                    expand(cat([top, terms - top]), 8), hot[pl.ds(lo * pairs, 8 * pairs), :]
                )
                sums = sums[:24] + sums[24:]
                for c in range(3):
                    wcat[lo:hi, c * bz : (c + 1) * bz] = (
                        sums[8 * c : 8 * c + 8] * cinv[lo:hi, :]
                    )
            parts = cat(split(wcat[...], 2))
        if not last:
            with scope("respond"):
                total = dots(0, base, mm(amat[0:base, :], parts))
                for d in range(len(DIRS)):
                    dsend[t, d] = total[d * outer : (d + 1) * outer]
                for d, (axis, sign) in enumerate(DIRS):

                    @pl.when(exists(axis, -sign))
                    def _():
                        answer(t, d, axis, sign).start()

        with scope("resid"):
            moved = mm(amat[base : base + (blocks if last else 2 * blocks), :], parts)
            near = moved[:blocks]
            resid = jnp.sum(lanes_sum(near * near * first_col), axis=1, keepdims=True)
            rrecv[mine] = jnp.where(lane == t, resid, rrecv[mine])
        if last:
            energy = jnp.sum(squares, axis=1, keepdims=True)
            rrecv[mine] = jnp.where(lane == SWEEPS, energy, rrecv[mine])
            to_all(rrecv.at[mine], rs_sem, rr_sem)
            with scope("join"):
                row = lax.broadcasted_iota(i32, (lines, 2 * blocks), 0).astype(f32)
                spread = jnp.where(row == two, 1.0, 0.0).astype(bf16)
                before = mm(spread, cat(split(acc[...], 2)))
                ahead = mm(spread, parts)
                for c in range(3):
                    pos_v[c] = pos_v[c] + before[:, c * bz : (c + 1) * bz].reshape(bx, by, bz)
                    out_ref[c] = ahead[:, c * bz : (c + 1) * bz].reshape(bx, by, bz)
            with scope("last_wait"):
                others = rrecv.at[pl.ds(0, devices - 1)]
                pltpu.make_async_copy(others, others, rr_sem).wait()
                energy = jnp.sum(rrecv[...], axis=0)[:, SWEEPS : SWEEPS + 1]
        else:
            with scope("step"):
                step = dots(base, 2 * blocks, moved)
                step = step[:blocks] + step[blocks:]
            with scope("energy_wait"):
                others = erecv.at[t, pl.ds(0, devices - 1)]
                pltpu.make_async_copy(others, others, er_sem.at[t]).wait()
                energy = jnp.sum(jnp.sum(erecv[t], axis=0), axis=1, keepdims=True)
        scale = 1.0 / (1.0 + energy / (blocks * pairs * devices))
        track[0:1, :] = jnp.where(lane == t, energy, track[0:1, :])
        track[1:2, :] = jnp.where(lane == t, scale, track[1:2, :])
        if last:
            for c in range(3):
                out_ref[c] = pos_v[c] + jnp.broadcast_to(scale[:, None], (1, 1, 1)) * out_ref[c]
            return
        with scope("answer_wait"):
            for d, (axis, sign) in enumerate(DIRS):

                @pl.when(exists(axis, sign))
                def _():
                    answer(t, d, axis, sign).wait_recv()

        more = drecv[t, 0]
        for d in range(1, len(DIRS)):
            more = more + drecv[t, d]
        acc[...] = acc[...] + scale * wcat[...]
        gap[0:outer, :] = gap[0:outer, :] + scale * step[:outer]
        gap[pl.ds(outer, outer), :] = gap[pl.ds(outer, outer), :] + scale * (step[outer:] + more)

    def body(t, carry):
        sweep(t, False)
        return carry

    lax.fori_loop(0, SWEEPS - 1, body, 0)
    sweep(SWEEPS - 1, True)

    with scope("end"):
        for d, (axis, sign) in enumerate(DIRS):

            @pl.when(exists(axis, sign))
            def _():
                for i in range(3):
                    ask(i, d, axis, sign).wait_send()

            @pl.when(exists(axis, -sign))
            def _():
                give(d, axis, sign).wait_send()
                for t in range(SWEEPS - 1):
                    answer(t, d, axis, sign).wait_send()

        for t in range(SWEEPS - 1):
            ref = erecv.at[t, pl.ds(0, devices - 1)]
            pltpu.make_async_copy(ref, ref, es_sem.at[t]).wait()
        others = rrecv.at[pl.ds(0, devices - 1)]
        pltpu.make_async_copy(others, others, rs_sem).wait()
        energy, scale = track[0:1, :], track[1:2, :]
        resid = jnp.sum(rrecv[...], axis=0)
        n = hist_ref.shape[1]
        hist_ref[0:1, :] = jnp.sqrt(1.0 + energy / (blocks * pairs))[:, :n]
        hist_ref[1:2, :] = jnp.sqrt(1.0 + scale * scale * resid / (bx * by * bz))[:, :n]


def local(sizes, positions, pair_node, pair_line, pair_far, far_line, pair_geom, live_blocks):
    blocks, pairs = pair_node.shape[3:]
    blk = positions.shape[1:]
    bx, by, bz = blk
    devices = sizes[0] * sizes[1] * sizes[2]
    outer = blocks // 2
    ndir = len(DIRS)
    rows = 2 * blocks + ndir * outer
    dma = pltpu.SemaphoreType.DMA
    vmem = pl.BlockSpec(memory_space=pltpu.VMEM)
    return pl.pallas_call(
        functools.partial(kernel, sizes, blk),
        out_shape=(
            jax.ShapeDtypeStruct(positions.shape, f32),
            jax.ShapeDtypeStruct((2, SWEEPS), f32),
        ),
        in_specs=[pl.BlockSpec(memory_space=pl.ANY)] * 7,
        out_specs=(vmem, vmem),
        scratch_shapes=[
            pltpu.VMEM(positions.shape, f32),
            pltpu.VMEM((blocks, pairs), i32),
            pltpu.VMEM((blocks, pairs), i32),
            pltpu.VMEM((blocks, 4, pairs), f32),
            pltpu.VMEM((1, blocks), i32),
            pltpu.VMEM((1, blocks), i32),
            pltpu.VMEM((1, 1), i32),
            pltpu.VMEM((ndir, outer, pairs), i32),
            pltpu.VMEM((ndir, 1, blocks), i32),
            pltpu.VMEM((ndir, outer, 4, pairs), f32),
            pltpu.VMEM((3, 3, bx * by, bz), bf16),
            pltpu.VMEM((blocks * pairs, bz), bf16),
            pltpu.VMEM((rows, 2 * blocks), bf16),
            pltpu.VMEM((3, rows, pairs), f32),
            pltpu.VMEM((rows, pairs), i32),
            pltpu.VMEM((rows, pairs), i32),
            pltpu.VMEM((blocks, bz), f32),
            pltpu.VMEM((blocks, pairs), f32),
            pltpu.VMEM((blocks, 3 * bz), f32),
            pltpu.VMEM((blocks, 3 * bz), f32),
            pltpu.VMEM((8, 128), f32),
            pltpu.VMEM((ndir, 3, outer, pairs), f32),
            pltpu.VMEM((ndir, 3, outer, pairs), f32),
            pltpu.VMEM((SWEEPS - 1, ndir, outer, pairs), f32),
            pltpu.VMEM((SWEEPS - 1, ndir, outer, pairs), f32),
            pltpu.VMEM((SWEEPS - 1, devices, 1, 128), f32),
            pltpu.VMEM((devices, 1, 128), f32),
            dma((7,)),
            dma((3, ndir)),
            dma((3, ndir)),
            dma((ndir,)),
            dma((ndir,)),
            dma((SWEEPS - 1, ndir)),
            dma((SWEEPS - 1, ndir)),
            dma((SWEEPS - 1,)),
            dma((SWEEPS - 1,)),
            dma,
            dma,
            pltpu.SemaphoreType.REGULAR,
            pltpu.SemaphoreType.REGULAR,
        ],
        compiler_params=pltpu.CompilerParams(collective_id=0, has_side_effects=True),
    )(live_blocks, pair_node, pair_line, pair_far, far_line, pair_geom, positions)


def solution(mesh):
    sizes = tuple(mesh.shape[a] for a in AXES)
    return jax.shard_map(
        functools.partial(local, sizes),
        mesh=mesh,
        in_specs=(
            P(None, "gx", "gy", "gz"),
            P("gx", "gy", "gz", None, None),
            P("gx", "gy", "gz", None),
            P("gx", "gy", "gz", None, None),
            P("gx", "gy", "gz", None),
            P("gx", "gy", "gz", None, None, None),
            P("gx", "gy", "gz"),
        ),
        out_specs=(P(None, "gx", "gy", "gz"), P()),
        check_vma=False,
    )
```

time: 69.4 us -> 51.9 us (0.75)
  Pallas kernels: 67.9 us -> 47.8 us
  local copies, waits for them, and re-layouts: 0 us -> 2.63 us
    pallas_call x1, Pallas kernels: 64.7 us -> 47.8 us  [local(): pl.pallas_call(functools.partial(kernel, sizes, blk), out_shape=(jax.Shap...]
    pallas_call x1 -> x0, Pallas kernels: 3.24 us -> none  [local(): pl.pallas_call(finish, grid=(3,), out_shape=(jax.ShapeDtypeStruct(positio...]
    unnamed x0 -> x4, local copies, waits for them, and re-layouts: none -> 2.63 us
where the time goes in v1:
time: 51.9 us; the launch traced here: 51.8 us
  Pallas kernels  47.8 us (92%)
  local copies, waits for them, and re-layouts  2.63 us (5%)
  between operations  1.3 us (3%)
    pallas_call x1, Pallas kernels, local(): pl.pallas_call(functools.partial(kernel, sizes, blk), out_shape=(jax.Shap...  47.8 us
    unnamed x4, local copies, waits for them, and re-layouts  2.63 us

profile of v1, /device:TPU:1, one launch (start us, length us, event | category | flops | bytes accessed | tf_op | source)
XLA Modules:
  0.0 51.8 jit_solution(6870195490449214072)
XLA Ops:
  1.3 47.8 %shard_map.86 = (f32[3,16,16,256]{3,2,1,0:T(8,128)}, f32[2,5]{1,0:T(2,128)}) custom-call(s32[1,1,1]{2,1,0:T(1,128)S(6)} %copy.11.live_hbm, s32[1,1,1,32,256]{4,3,2,1,0:T(8,128)} %node_hbm.1, s32[1,1,1,32]{3,2,1,0:T(1,128)} %line_hbm.1, s32[1,1,1,32,256]{4,3,2,1,0:T(8,128)} %far_hbm.1, s32[1,1,1,32]{3,2,1,0:T(1,128)} %farline_hbm.1, ...), custom_call_target="tpu_custom_call" | custom-call | tf_op jit(solution)/shard_map/pallas_call | solution.py:548
  49.1 0.0 copy-start
  49.1 2.1 %copy.12 = f32[3,16,16,256]{3,2,1,0:T(8,128)} copy(f32[3,16,16,256]{3,2,1,0:T(8,128)} %get-tuple-element.4) | data formatting | bytes 1572864
  51.2 0.0 copy-done
  51.2 0.6 %copy.13 = f32[2,5]{1,0:T(2,128)} copy(f32[2,5]{1,0:T(2,128)S(1)} %copy-done) | data formatting | bytes 80
Async XLA Ops:
  49.1 2.1 %copy-start = (f32[2,5]{1,0:T(2,128)S(1)}, f32[2,5]{1,0:T(2,128)}, u32[]{:S(2)}) copy-start(f32[2,5]{1,0:T(2,128)} %get-tuple-element.5) | copy-start | bytes 124

commit v2 on v1

--- a/solution.py
+++ b/solution.py
@@ -85,6 +85,8 @@
     half_ref,
     cinv,
     gap,
+    depth_ref,
+    delta,
     wcat,
     acc,
     track,
@@ -93,18 +95,14 @@
     dsend,
     drecv,
     erecv,
-    rrecv,
     in_sem,
     qs_sem,
     qr_sem,
-    vs_sem,
+    as_sem,
     vr_sem,
-    ds_sem,
     dr_sem,
     es_sem,
     er_sem,
-    rs_sem,
-    rr_sem,
     plane_sem,
     all_sem,
 ):
@@ -167,7 +165,7 @@
         return pltpu.make_async_remote_copy(
             src_ref=asks[i][0],
             dst_ref=asks[i][1].at[d],
-            send_sem=qs_sem.at[i, d],
+            send_sem=qs_sem.at[i % 2, d],
             recv_sem=qr_sem.at[i, d],
             device_id=neighbour(axis, sign),
             device_id_type=MESH,
@@ -239,18 +237,21 @@
 
     def place(row, line, node):
         n = line.shape[0]
-        amat[pl.ds(row, n), :] = jnp.where(line == two, 1.0, 0.0).astype(bf16)
         idx = node.astype(i32)
         low = lax.bitwise_and(idx, 127)
         half = lax.shift_right_logical(idx, 7)
-        low_ref[pl.ds(row, n), :] = low
-        half_ref[pl.ds(row, n), :] = half
         own = jnp.where(line == lane_line, 1.0, 0.0).astype(bf16)
-        out = []
-        for c in range(3):
+
+        def value(c):
             vals = mm(own, ppart[c, 0]) + mm(own, ppart[c, 1]) + mm(own, ppart[c, 2])
-            out.append(take_lanes(vals, low, half))
-        return out
+            return take_lanes(vals, low, half)
+
+        def keep():
+            amat[pl.ds(row, n), :] = jnp.where(line == two, 1.0, 0.0).astype(bf16)
+            low_ref[pl.ds(row, n), :] = low
+            half_ref[pl.ds(row, n), :] = half
+
+        return value, keep
 
     with scope("known"):
         pl.semaphore_wait(plane_sem, ny - 1)
@@ -265,11 +266,11 @@
                 ask(1, d, axis, sign).wait_recv()
                 ask(0, d, axis, sign).wait_recv()
 
-    def give(d, axis, sign):
+    def give(c, d, axis, sign):
         return pltpu.make_async_remote_copy(
-            src_ref=vsend.at[d],
-            dst_ref=vrecv.at[d],
-            send_sem=vs_sem.at[d],
+            src_ref=vsend.at[d, c],
+            dst_ref=vrecv.at[d, c],
+            send_sem=as_sem.at[d],
             recv_sem=vr_sem.at[d],
             device_id=neighbour(axis, -sign),
             device_id_type=MESH,
@@ -286,16 +287,18 @@
             asked_node.append(z)
             asked_ok.append(jnp.where(ok, 1.0, 0.0))
         asked_ok = cat(asked_ok)
-        vals = place(0, cat(asked_line), cat(asked_node))
+        value, keep = place(0, cat(asked_line), cat(asked_node))
         for c in range(3):
-            got = vals[c] * asked_ok
+            got = value(c) * asked_ok
             for d in range(len(DIRS)):
                 vsend[d, c] = got[d * outer : (d + 1) * outer]
-        for d, (axis, sign) in enumerate(DIRS):
-
-            @pl.when(exists(axis, -sign))
-            def _():
-                give(d, axis, sign).start()
+            for d, (axis, sign) in enumerate(DIRS):
+
+                @pl.when(exists(axis, -sign))
+                def _():
+                    give(c, d, axis, sign).start()
+
+        keep()
 
     with scope("counts"):
         live = jnp.broadcast_to(live_v[...], (blocks, pairs))
@@ -326,18 +329,20 @@
         code = column(farline_v[...].astype(f32), 0, blocks)
         line, z, ok = located(code, far_v[...].astype(f32), (0, 0, 0))
         here = jnp.where(ok, 1.0, 0.0)
-        vals = place(base, cat([line_col, line]), cat([node_v[...].astype(f32), z]))
+        value, keep = place(base, cat([line_col, line]), cat([node_v[...].astype(f32), z]))
         start = -geom_v[:, 3, :]
         for c in range(3):
             g = geom_v[:, c, :]
             away = -(g * here)
             geo[c, pl.ds(base, blocks), :] = g
             geo[c, pl.ds(base + blocks, blocks), :] = away
-            start += g * vals[c][:blocks] + away * vals[c][blocks:]
+            vals = value(c)
+            start += g * vals[:blocks] + away * vals[blocks:]
+        keep()
         gap[...] = start
         acc[...] = jnp.zeros_like(acc)
+        wcat[...] = jnp.zeros_like(wcat)
         track[...] = jnp.zeros_like(track)
-        rrecv[mine] = jnp.zeros((1, 128), f32)
 
     with scope("geo"):
         for d, (axis, sign) in enumerate(DIRS):
@@ -357,7 +362,7 @@
 
             @pl.when(exists(axis, sign))
             def _():
-                give(d, axis, sign).wait_recv()
+                pltpu.make_async_copy(vrecv.at[d], vrecv.at[d], vr_sem.at[d]).wait()
 
         more = jnp.zeros((outer, pairs), f32)
         for c in range(3):
@@ -371,8 +376,8 @@
         return pltpu.make_async_remote_copy(
             src_ref=dsend.at[t, d],
             dst_ref=drecv.at[t, d],
-            send_sem=ds_sem.at[t, d],
-            recv_sem=dr_sem.at[t, d],
+            send_sem=as_sem.at[d],
+            recv_sem=dr_sem.at[lax.rem(t, 2), d],
             device_id=neighbour(axis, -sign),
             device_id_type=MESH,
         )
@@ -388,16 +393,25 @@
         reverse=True,
     )
 
-    def to_all(ref, send_sem, recv_sem):
+    def to_all(t):
+        ref = erecv.at[t, mine]
         for off in everyone:
             pltpu.make_async_remote_copy(
                 src_ref=ref,
                 dst_ref=ref,
-                send_sem=send_sem,
-                recv_sem=recv_sem,
+                send_sem=es_sem,
+                recv_sem=er_sem.at[lax.rem(t, 2)],
                 device_id=at_offset(off),
                 device_id_type=MESH,
             ).start()
+
+    def from_all(t):
+        others = erecv.at[t, pl.ds(0, devices - 1)]
+        pltpu.make_async_copy(others, others, er_sem.at[lax.rem(t, 2)]).wait()
+        rows = [erecv[t, i] for i in range(devices)]
+        while len(rows) > 1:
+            rows = [a + b for a, b in zip(rows[::2], rows[1::2])] + rows[len(rows) & ~1 :]
+        return rows[0]
 
     def lanes_sum(x):
         x = jnp.sum(x, axis=0, keepdims=True)
@@ -418,76 +432,55 @@
             )
         return total
 
-    def sweep(t, last):
-        with scope("energy"):
-            depth = jnp.where(live_rows, jnp.maximum(-gap[...], 0.0), 0.0)
-            squares = lanes_sum(depth * depth)
-            if not last:
-                erecv[t, mine] = squares
-                to_all(erecv.at[t, mine], es_sem.at[t], er_sem.at[t])
-        with scope("scatter"):
-            for g in range(blocks // 8):
-                lo, hi = 8 * g, 8 * g + 8
-                terms = cat(
-                    [depth[lo:hi] * geo[c, base + lo : base + hi] for c in range(3)]
-                )
-                top = terms.astype(bf16).astype(f32)
-                sums = mm(
-                    expand(cat([top, terms - top]), 8), hot[pl.ds(lo * pairs, 8 * pairs), :]
-                )
-                sums = sums[:24] + sums[24:]
-                for c in range(3):
-                    wcat[lo:hi, c * bz : (c + 1) * bz] = (
-                        sums[8 * c : 8 * c + 8] * cinv[lo:hi, :]
-                    )
-            parts = cat(split(wcat[...], 2))
-        if not last:
-            with scope("respond"):
-                total = dots(0, base, mm(amat[0:base, :], parts))
-                for d in range(len(DIRS)):
-                    dsend[t, d] = total[d * outer : (d + 1) * outer]
-                for d, (axis, sign) in enumerate(DIRS):
-
-                    @pl.when(exists(axis, -sign))
-                    def _():
-                        answer(t, d, axis, sign).start()
-
-        with scope("resid"):
-            moved = mm(amat[base : base + (blocks if last else 2 * blocks), :], parts)
-            near = moved[:blocks]
-            resid = jnp.sum(lanes_sum(near * near * first_col), axis=1, keepdims=True)
-            rrecv[mine] = jnp.where(lane == t, resid, rrecv[mine])
-        if last:
-            energy = jnp.sum(squares, axis=1, keepdims=True)
-            rrecv[mine] = jnp.where(lane == SWEEPS, energy, rrecv[mine])
-            to_all(rrecv.at[mine], rs_sem, rr_sem)
-            with scope("join"):
-                row = lax.broadcasted_iota(i32, (lines, 2 * blocks), 0).astype(f32)
-                spread = jnp.where(row == two, 1.0, 0.0).astype(bf16)
-                before = mm(spread, cat(split(acc[...], 2)))
-                ahead = mm(spread, parts)
-                for c in range(3):
-                    pos_v[c] = pos_v[c] + before[:, c * bz : (c + 1) * bz].reshape(bx, by, bz)
-                    out_ref[c] = ahead[:, c * bz : (c + 1) * bz].reshape(bx, by, bz)
-            with scope("last_wait"):
-                others = rrecv.at[pl.ds(0, devices - 1)]
-                pltpu.make_async_copy(others, others, rr_sem).wait()
-                energy = jnp.sum(rrecv[...], axis=0)[:, SWEEPS : SWEEPS + 1]
-        else:
-            with scope("step"):
-                step = dots(base, 2 * blocks, moved)
-                step = step[:blocks] + step[blocks:]
-            with scope("energy_wait"):
-                others = erecv.at[t, pl.ds(0, devices - 1)]
-                pltpu.make_async_copy(others, others, er_sem.at[t]).wait()
-                energy = jnp.sum(jnp.sum(erecv[t], axis=0), axis=1, keepdims=True)
-        scale = 1.0 / (1.0 + energy / (blocks * pairs * devices))
+    def depths():
+        depth = jnp.where(live_rows, jnp.maximum(-gap[...], 0.0), 0.0)
+        depth_ref[...] = depth
+        return lanes_sum(depth * depth)
+
+    def scatter():
+        for g in range(blocks // 8):
+            lo, hi = 8 * g, 8 * g + 8
+            depth = depth_ref[lo:hi, :]
+            terms = cat([depth * geo[c, base + lo : base + hi] for c in range(3)])
+            top = terms.astype(bf16).astype(f32)
+            sums = mm(expand(cat([top, terms - top]), 8), hot[pl.ds(lo * pairs, 8 * pairs), :])
+            sums = sums[:24] + sums[24:]
+            for c in range(3):
+                wcat[lo:hi, c * bz : (c + 1) * bz] = sums[8 * c : 8 * c + 8] * cinv[lo:hi, :]
+        return cat(split(wcat[...], 2))
+
+    def residual(near):
+        return jnp.sum(lanes_sum(near * near * first_col), axis=1, keepdims=True)
+
+    def note(t, energy, scale):
         track[0:1, :] = jnp.where(lane == t, energy, track[0:1, :])
         track[1:2, :] = jnp.where(lane == t, scale, track[1:2, :])
-        if last:
-            for c in range(3):
-                out_ref[c] = pos_v[c] + jnp.broadcast_to(scale[:, None], (1, 1, 1)) * out_ref[c]
-            return
+        acc[...] = acc[...] + scale * wcat[...]
+
+    def ratio(energy):
+        return 1.0 / (1.0 + energy / (blocks * pairs * devices))
+
+    def sweep(t, energy, last):
+        with scope("note"):
+            note(t - 1, energy, ratio(energy))
+        with scope("scatter"):
+            parts = scatter()
+        with scope("respond"):
+            total = dots(0, base, mm(amat[0:base, :], parts))
+            for d in range(len(DIRS)):
+                dsend[t, d] = total[d * outer : (d + 1) * outer]
+            for d, (axis, sign) in enumerate(DIRS):
+
+                @pl.when(exists(axis, -sign))
+                def _():
+                    answer(t, d, axis, sign).start()
+
+        with scope("step"):
+            moved = mm(amat[base : base + 2 * blocks, :], parts)
+            resid = residual(moved[:blocks])
+            track[2:3, :] = jnp.where(lane == t, resid, track[2:3, :])
+            step = dots(base, 2 * blocks, moved)
+            delta[...] = step[:blocks] + step[blocks:]
         with scope("answer_wait"):
             for d, (axis, sign) in enumerate(DIRS):
 
@@ -495,44 +488,84 @@
                 def _():
                     answer(t, d, axis, sign).wait_recv()
 
-        more = drecv[t, 0]
-        for d in range(1, len(DIRS)):
-            more = more + drecv[t, d]
-        acc[...] = acc[...] + scale * wcat[...]
-        gap[0:outer, :] = gap[0:outer, :] + scale * step[:outer]
-        gap[pl.ds(outer, outer), :] = gap[pl.ds(outer, outer), :] + scale * (step[outer:] + more)
-
-    def body(t, carry):
-        sweep(t, False)
-        return carry
-
-    lax.fori_loop(0, SWEEPS - 1, body, 0)
-    sweep(SWEEPS - 1, True)
-
+            more = drecv[t, 0]
+            for d in range(1, len(DIRS)):
+                more = more + drecv[t, d]
+            delta[pl.ds(outer, outer), :] = delta[pl.ds(outer, outer), :] + more
+        with scope("energy_wait"):
+            energy = jnp.sum(from_all(t), axis=1, keepdims=True)
+        with scope("energy"):
+            gap[...] = gap[...] + ratio(energy) * delta[...]
+            squares = depths()
+            if last:
+                return energy, squares
+            erecv[t + 1, mine] = squares
+            to_all(t + 1)
+        return energy
+
+    with scope("energy"):
+        erecv[0, mine] = depths()
+        to_all(0)
+
+    zero = jnp.zeros((1, 1), f32)
+    energy = lax.fori_loop(0, SWEEPS - 2, lambda t, energy: sweep(t, energy, False), zero)
+    energy, squares = sweep(SWEEPS - 2, energy, True)
+    end = SWEEPS - 1
+    with scope("scatter"):
+        note(end - 1, energy, ratio(energy))
+        parts = scatter()
+    with scope("resid"):
+        resid = residual(mm(amat[base : base + blocks, :], parts))
+        energy = jnp.sum(squares, axis=1, keepdims=True)
+        row = jnp.where(lane == end, resid, track[2:3, :])
+        erecv[end, mine] = jnp.where(lane == SWEEPS, energy, row)
+        to_all(end)
+    with scope("join"):
+        row = lax.broadcasted_iota(i32, (lines, 2 * blocks), 0).astype(f32)
+        spread = jnp.where(row == two, 1.0, 0.0).astype(bf16)
+        before = mm(spread, cat(split(acc[...], 2)))
+        ahead = mm(spread, parts)
+        for c in range(3):
+            pos_v[c] = pos_v[c] + before[:, c * bz : (c + 1) * bz].reshape(bx, by, bz)
+            out_ref[c] = ahead[:, c * bz : (c + 1) * bz].reshape(bx, by, bz)
+        for d, (axis, sign) in enumerate(DIRS):
+
+            @pl.when(exists(axis, sign))
+            def _():
+                sent = geo.at[0, pl.ds(0, 5 * outer)]
+                pltpu.make_async_copy(sent, sent, qs_sem.at[0, d]).wait()
+                ask(1, d, axis, sign).wait_send()
+
+            @pl.when(exists(axis, -sign))
+            def _():
+                sent = geo.at[0, pl.ds(0, (SWEEPS + 2) * outer)]
+                pltpu.make_async_copy(sent, sent, as_sem.at[d]).wait()
+
+    with scope("last_wait"):
+        sums = from_all(end)
     with scope("end"):
-        for d, (axis, sign) in enumerate(DIRS):
-
-            @pl.when(exists(axis, sign))
-            def _():
-                for i in range(3):
-                    ask(i, d, axis, sign).wait_send()
-
-            @pl.when(exists(axis, -sign))
-            def _():
-                give(d, axis, sign).wait_send()
-                for t in range(SWEEPS - 1):
-                    answer(t, d, axis, sign).wait_send()
-
-        for t in range(SWEEPS - 1):
-            ref = erecv.at[t, pl.ds(0, devices - 1)]
-            pltpu.make_async_copy(ref, ref, es_sem.at[t]).wait()
-        others = rrecv.at[pl.ds(0, devices - 1)]
-        pltpu.make_async_copy(others, others, rs_sem).wait()
-        energy, scale = track[0:1, :], track[1:2, :]
-        resid = jnp.sum(rrecv[...], axis=0)
+        energy = sums[:, SWEEPS : SWEEPS + 1]
+        scale = ratio(energy)
+        for c in range(3):
+            out_ref[c] = pos_v[c] + jnp.broadcast_to(scale[:, None], (1, 1, 1)) * out_ref[c]
         n = hist_ref.shape[1]
-        hist_ref[0:1, :] = jnp.sqrt(1.0 + energy / (blocks * pairs))[:, :n]
-        hist_ref[1:2, :] = jnp.sqrt(1.0 + scale * scale * resid / (bx * by * bz))[:, :n]
+        energies = jnp.where(lane == end, energy, track[0:1, :])
+        scales = jnp.where(lane == end, scale, track[1:2, :])
+        hist_ref[0:1, :] = jnp.sqrt(1.0 + energies / (blocks * pairs))[:, :n]
+        hist_ref[1:2, :] = jnp.sqrt(1.0 + scales * scales * sums / (bx * by * bz))[:, :n]
+        sent = erecv.at[pl.ds(0, SWEEPS), pl.ds(0, devices - 1)]
+        pltpu.make_async_copy(sent, sent, es_sem).wait()
+
+
+def finish(moved, hist, out_hbm, hist_hbm, sem):
+    copies = [
+        pltpu.make_async_copy(moved, out_hbm, sem.at[0]),
+        pltpu.make_async_copy(hist, hist_hbm, sem.at[1]),
+    ]
+    for copy in copies:
+        copy.start()
+    for copy in copies:
+        copy.wait()
 
 
 def local(sizes, positions, pair_node, pair_line, pair_far, far_line, pair_geom, live_blocks):
@@ -545,13 +578,13 @@
     rows = 2 * blocks + ndir * outer
     dma = pltpu.SemaphoreType.DMA
     vmem = pl.BlockSpec(memory_space=pltpu.VMEM)
-    return pl.pallas_call(
+    moved, hist = pl.pallas_call(
         functools.partial(kernel, sizes, blk),
         out_shape=(
-            jax.ShapeDtypeStruct(positions.shape, f32),
-            jax.ShapeDtypeStruct((2, SWEEPS), f32),
+            pltpu.VMEM(positions.shape, f32),
+            pltpu.VMEM((2, SWEEPS), f32),
         ),
-        in_specs=[pl.BlockSpec(memory_space=pl.ANY)] * 7,
+        in_specs=[pl.BlockSpec(memory_space=pltpu.HBM)] * 7,
         out_specs=(vmem, vmem),
         scratch_shapes=[
             pltpu.VMEM(positions.shape, f32),
@@ -572,6 +605,8 @@
             pltpu.VMEM((rows, pairs), i32),
             pltpu.VMEM((blocks, bz), f32),
             pltpu.VMEM((blocks, pairs), f32),
+            pltpu.VMEM((blocks, pairs), f32),
+            pltpu.VMEM((blocks, pairs), f32),
             pltpu.VMEM((blocks, 3 * bz), f32),
             pltpu.VMEM((blocks, 3 * bz), f32),
             pltpu.VMEM((8, 128), f32),
@@ -579,24 +614,33 @@
             pltpu.VMEM((ndir, 3, outer, pairs), f32),
             pltpu.VMEM((SWEEPS - 1, ndir, outer, pairs), f32),
             pltpu.VMEM((SWEEPS - 1, ndir, outer, pairs), f32),
-            pltpu.VMEM((SWEEPS - 1, devices, 1, 128), f32),
-            pltpu.VMEM((devices, 1, 128), f32),
+            pltpu.VMEM((SWEEPS, devices, 1, 128), f32),
             dma((7,)),
-            dma((3, ndir)),
+            dma((2, ndir)),
             dma((3, ndir)),
             dma((ndir,)),
             dma((ndir,)),
-            dma((SWEEPS - 1, ndir)),
-            dma((SWEEPS - 1, ndir)),
-            dma((SWEEPS - 1,)),
-            dma((SWEEPS - 1,)),
+            dma((2, ndir)),
             dma,
-            dma,
+            dma((2,)),
             pltpu.SemaphoreType.REGULAR,
             pltpu.SemaphoreType.REGULAR,
         ],
         compiler_params=pltpu.CompilerParams(collective_id=0, has_side_effects=True),
     )(live_blocks, pair_node, pair_line, pair_far, far_line, pair_geom, positions)
+    return pl.pallas_call(
+        finish,
+        out_shape=(
+            jax.ShapeDtypeStruct(positions.shape, f32),
+            jax.ShapeDtypeStruct((2, SWEEPS), f32),
+        ),
+        in_specs=[vmem, vmem],
+        out_specs=(pl.BlockSpec(memory_space=pl.ANY),) * 2,
+        scratch_shapes=[dma((2,))],
+    )(
+        pltpu.with_memory_space_constraint(moved, pltpu.VMEM),
+        pltpu.with_memory_space_constraint(hist, pltpu.VMEM),
+    )
 
 
 def solution(mesh):

time: 51.9 us -> 48.3 us (0.931)
  local copies, waits for them, and re-layouts: 2.63 us -> 0 us
  Pallas kernels: 47.8 us -> 46.9 us
    unnamed x4 -> x0, local copies, waits for them, and re-layouts: 2.63 us -> none
    pallas_call x1 -> x2, Pallas kernels: 47.8 us -> 46.9 us  [the longest x1 46 us: local(): pl.pallas_call(functools.partial(kernel, sizes, blk), out_shape=(pltpu.VM...]
where the time goes in v2:
time: 48.3 us; the launch traced here: 48.2 us
  Pallas kernels  46.9 us (97%)
  between operations  1.29 us (3%)
    pallas_call x1, Pallas kernels, local(): pl.pallas_call(functools.partial(kernel, sizes, blk), out_shape=(pltpu.VM...  46 us

profile of v2, /device:TPU:1, one launch (start us, length us, event | category | flops | bytes accessed | tf_op | source)
XLA Modules:
  0.0 48.2 jit_solution(5273030071544800384)
XLA Ops:
  1.3 46.0 %shard_map.86 = (f32[3,16,16,256]{3,2,1,0:T(8,128)S(1)}, f32[2,5]{1,0:T(2,128)S(1)}) custom-call(s32[1,1,1]{2,1,0:T(1,128)S(6)} %copy.9.live_hbm, s32[1,1,1,32,256]{4,3,2,1,0:T(8,128)} %node_hbm.1, s32[1,1,1,32]{3,2,1,0:T(1,128)} %line_hbm.1, s32[1,1,1,32,256]{4,3,2,1,0:T(8,128)} %far_hbm.1, s32[1,1,1,32]{3,2,1,0:T(1,128)} %farline_hbm.1, ...), custom_call_target="tpu_custom_call" | custom-call | tf_op jit(solution)/shard_map/pallas_call | solution.py:581
  47.3 0.9 %shard_map.87 = (f32[3,16,16,256]{3,2,1,0:T(8,128)}, f32[2,5]{1,0:T(2,128)}) custom-call(f32[3,16,16,256]{3,2,1,0:T(8,128)S(1)} %get-tuple-element.4.moved, f32[2,5]{1,0:T(2,128)S(1)} %get-tuple-element.5.hist), custom_call_target="tpu_custom_call" | custom-call | tf_op jit(solution)/shard_map/pallas_call | solution.py:631

commit v3 on v2

--- a/solution.py
+++ b/solution.py
@@ -15,6 +15,7 @@
 MESH = pl.DeviceIdType.MESH
 f32 = jnp.float32
 bf16 = jnp.bfloat16
+f8 = jnp.float8_e4m3fn
 i32 = jnp.int32
 DIRS = [(a, s) for a in (1, 0, 2) for s in (1, -1)]
 
@@ -34,7 +35,7 @@
 
 
 def mm(a, b):
-    return jnp.dot(a, b, preferred_element_type=f32)
+    return lax.dot_general(a, b, (((1,), (0,)), ((), ())), preferred_element_type=f32)
 
 
 def cat(parts):
@@ -78,6 +79,7 @@
     rline,
     rgeom,
     ppart,
+    spare,
     hot,
     amat,
     geo,
@@ -98,13 +100,10 @@
     in_sem,
     qs_sem,
     qr_sem,
-    as_sem,
     vr_sem,
-    dr_sem,
     es_sem,
     er_sem,
-    plane_sem,
-    all_sem,
+    know_sem,
 ):
     nx, ny, nz = sizes
     bx, by, bz = blk
@@ -130,11 +129,15 @@
     def along(axis):
         return [tuple(o if a == axis else 0 for a in range(3)) for o in range(1, sizes[axis])]
 
+    def tell(sem, peers):
+        for off in peers:
+            pl.semaphore_signal(sem, inc=1, device_id=at_offset(off), device_id_type=MESH)
+
+    close = along(2) + along(1) + along(0)
+
     with scope("entry"):
         barrier = pltpu.get_barrier_semaphore()
-        close = along(2) + along(1) + along(0)
-        for off in close:
-            pl.semaphore_signal(barrier, inc=1, device_id=at_offset(off), device_id_type=MESH)
+        tell(barrier, close)
         loads = [
             pltpu.make_async_copy(src, dst, in_sem.at[i])
             for i, (src, dst) in enumerate(
@@ -153,6 +156,7 @@
             load.start()
         loads[0].wait()
         loads[1].wait()
+    with scope("barrier"):
         pl.semaphore_wait(barrier, len(close))
 
     asks = [
@@ -179,8 +183,7 @@
                 ask(1, d, axis, sign).start()
                 ask(0, d, axis, sign).start()
 
-        for off in along(1):
-            pl.semaphore_signal(plane_sem, inc=1, device_id=at_offset(off), device_id_type=MESH)
+        tell(know_sem.at[0], along(1))
         loads[2].wait()
         for d, (axis, sign) in enumerate(DIRS):
 
@@ -214,7 +217,7 @@
         for b in range(blocks):
             hot[pl.ds(b * pairs, pairs), :] = jnp.where(
                 node_t[:, b : b + 1] == lane_node, 1.0, 0.0
-            ).astype(bf16)
+            ).astype(f8)
 
     row_line = line_v[...].astype(f32)
     two = jnp.concatenate([row_line, row_line], axis=1)
@@ -225,71 +228,87 @@
         l = lax.broadcasted_iota(i32, (n, blocks), 1)
         return jnp.sum(jnp.where(l == r + first, row, 0.0), axis=1, keepdims=True)
 
-    def located(code, zpos, shift):
+    def located(code, shift):
         e = jnp.floor((code + 0.5) / (by + 2 * RIM))
         f = code - e * (by + 2 * RIM)
         e = e - (RIM + shift[0] * bx)
         f = f - (RIM + shift[1] * by)
-        z = zpos - (RIM + shift[2] * bz)
-        ok_line = (e >= 0) & (e < bx) & (f >= 0) & (f < by)
-        ok = ok_line & (z >= 0) & (z < bz)
-        return jnp.where(ok_line, e * by + f, -1.0), jnp.where(ok, z, 0.0), ok
-
-    def place(row, line, node):
+        inside = (e >= 0) & (e < bx) & (f >= 0) & (f < by)
+        return jnp.where(inside, e * by + f, -1.0), inside
+
+    def depth_at(place, inside, shift):
+        z = place - (RIM + shift[2] * bz)
+        here = inside & (z >= 0) & (z < bz)
+        return jnp.where(here, z, 0), jnp.where(here, 1.0, 0.0)
+
+    def halves(node):
+        return lax.bitwise_and(node, 127), lax.shift_right_logical(node, 7)
+
+    def values(dst, line):
+        own = jnp.where(line == lane_line, 1.0, 0.0).astype(bf16)
+        for c in range(3):
+            dst[c, 0 : line.shape[0]] = (
+                mm(own, ppart[c, 0]) + mm(own, ppart[c, 1]) + mm(own, ppart[c, 2])
+            )
+
+    def keep(row, line, low, half):
         n = line.shape[0]
-        idx = node.astype(i32)
-        low = lax.bitwise_and(idx, 127)
-        half = lax.shift_right_logical(idx, 7)
-        own = jnp.where(line == lane_line, 1.0, 0.0).astype(bf16)
-
-        def value(c):
-            vals = mm(own, ppart[c, 0]) + mm(own, ppart[c, 1]) + mm(own, ppart[c, 2])
-            return take_lanes(vals, low, half)
-
-        def keep():
-            amat[pl.ds(row, n), :] = jnp.where(line == two, 1.0, 0.0).astype(bf16)
-            low_ref[pl.ds(row, n), :] = low
-            half_ref[pl.ds(row, n), :] = half
-
-        return value, keep
+        amat[pl.ds(row, n), :] = jnp.where(line == two, 1.0, 0.0).astype(bf16)
+        low_ref[pl.ds(row, n), :] = low
+        half_ref[pl.ds(row, n), :] = half
 
     with scope("known"):
-        pl.semaphore_wait(plane_sem, ny - 1)
-        for off in along(2):
-            pl.semaphore_signal(all_sem, inc=1, device_id=at_offset(off), device_id_type=MESH)
-
-    with scope("ask_wait"):
-        for d, (axis, sign) in enumerate(DIRS):
-
-            @pl.when(exists(axis, -sign))
-            def _():
-                ask(1, d, axis, sign).wait_recv()
-                ask(0, d, axis, sign).wait_recv()
+        pl.semaphore_wait(know_sem.at[0], ny - 1)
+        tell(know_sem.at[1], along(2))
 
     def give(c, d, axis, sign):
         return pltpu.make_async_remote_copy(
             src_ref=vsend.at[d, c],
             dst_ref=vrecv.at[d, c],
-            send_sem=as_sem.at[d],
+            send_sem=qs_sem.at[1, d],
             recv_sem=vr_sem.at[d],
             device_id=neighbour(axis, -sign),
             device_id_type=MESH,
         )
 
-    with scope("give"):
-        asked_line, asked_node, asked_ok = [], [], []
+    with scope("line_wait"):
+        for d, (axis, sign) in enumerate(DIRS):
+
+            @pl.when(exists(axis, sign))
+            def _():
+                ask(1, d, axis, sign).wait_send()
+
+            @pl.when(exists(axis, -sign))
+            def _():
+                ask(1, d, axis, sign).wait_recv()
+
+    with scope("lines"):
+        shifts = []
+        asked_line, asked_in = [], []
         for d, (axis, sign) in enumerate(DIRS):
             shift = [0, 0, 0]
             shift[axis] = sign
-            code = column(rline[d].astype(f32), outer, outer)
-            line, z, ok = located(code, rfar[d].astype(f32), shift)
+            shifts.append(shift)
+            line, inside = located(column(rline[d].astype(f32), outer, outer), shift)
             asked_line.append(line)
-            asked_node.append(z)
-            asked_ok.append(jnp.where(ok, 1.0, 0.0))
-        asked_ok = cat(asked_ok)
-        value, keep = place(0, cat(asked_line), cat(asked_node))
+            asked_in.append(inside)
+        asked_line = cat(asked_line)
+        values(spare, asked_line)
+    with scope("far_wait"):
+        for d, (axis, sign) in enumerate(DIRS):
+
+            @pl.when(exists(axis, -sign))
+            def _():
+                ask(0, d, axis, sign).wait_recv()
+
+    with scope("give"):
+        found = [
+            depth_at(rfar[d], asked_in[d], shifts[d]) for d in range(len(DIRS))
+        ]
+        low, half = halves(cat([node for node, _ in found]))
+        asked_ok = cat([here for _, here in found])
         for c in range(3):
-            got = value(c) * asked_ok
+            got = take_lanes(spare[c], low, half) * asked_ok
             for d in range(len(DIRS)):
                 vsend[d, c] = got[d * outer : (d + 1) * outer]
             for d, (axis, sign) in enumerate(DIRS):
@@ -298,8 +317,8 @@
                 def _():
                     give(c, d, axis, sign).start()
 
-        keep()
-
+    with scope("keep"):
+        keep(0, asked_line, low, half)
     with scope("counts"):
         live = jnp.broadcast_to(live_v[...], (blocks, pairs))
         live_rows = lax.broadcasted_iota(i32, (blocks, pairs), 0) < live
@@ -326,19 +345,20 @@
         cinv[...] = RELAX / (1.0 + mm(jnp.where(same, 1.0, 0.0).astype(bf16), counts))
 
     with scope("own"):
-        code = column(farline_v[...].astype(f32), 0, blocks)
-        line, z, ok = located(code, far_v[...].astype(f32), (0, 0, 0))
-        here = jnp.where(ok, 1.0, 0.0)
-        value, keep = place(base, cat([line_col, line]), cat([node_v[...].astype(f32), z]))
+        line, inside = located(column(farline_v[...].astype(f32), 0, blocks), (0, 0, 0))
+        node, here = depth_at(far_v[...], inside, (0, 0, 0))
+        line = cat([line_col, line])
+        low, half = halves(cat([node_v[...], node]))
+        values(spare, line)
+        keep(base, line, low, half)
         start = -geom_v[:, 3, :]
         for c in range(3):
             g = geom_v[:, c, :]
             away = -(g * here)
             geo[c, pl.ds(base, blocks), :] = g
             geo[c, pl.ds(base + blocks, blocks), :] = away
-            vals = value(c)
+            vals = take_lanes(spare[c, 0 : 2 * blocks], low, half)
             start += g * vals[:blocks] + away * vals[blocks:]
-        keep()
         gap[...] = start
         acc[...] = jnp.zeros_like(acc)
         wcat[...] = jnp.zeros_like(wcat)
@@ -357,7 +377,7 @@
                 geo[c, rows, :] = -(rgeom[d, :, c, :] * asked_ok[rows])
 
     with scope("give_wait"):
-        pl.semaphore_wait(all_sem, nz - 1)
+        pl.semaphore_wait(know_sem.at[1], nz - 1)
         for d, (axis, sign) in enumerate(DIRS):
 
             @pl.when(exists(axis, sign))
@@ -376,8 +396,8 @@
         return pltpu.make_async_remote_copy(
             src_ref=dsend.at[t, d],
             dst_ref=drecv.at[t, d],
-            send_sem=as_sem.at[d],
-            recv_sem=dr_sem.at[lax.rem(t, 2), d],
+            send_sem=qs_sem.at[1, d],
+            recv_sem=qr_sem.at[lax.rem(t, 2), d],
             device_id=neighbour(axis, -sign),
             device_id_type=MESH,
         )
@@ -534,12 +554,11 @@
             def _():
                 sent = geo.at[0, pl.ds(0, 5 * outer)]
                 pltpu.make_async_copy(sent, sent, qs_sem.at[0, d]).wait()
-                ask(1, d, axis, sign).wait_send()
 
             @pl.when(exists(axis, -sign))
             def _():
                 sent = geo.at[0, pl.ds(0, (SWEEPS + 2) * outer)]
-                pltpu.make_async_copy(sent, sent, as_sem.at[d]).wait()
+                pltpu.make_async_copy(sent, sent, qs_sem.at[1, d]).wait()
 
     with scope("last_wait"):
         sums = from_all(end)
@@ -598,7 +617,8 @@
             pltpu.VMEM((ndir, 1, blocks), i32),
             pltpu.VMEM((ndir, outer, 4, pairs), f32),
             pltpu.VMEM((3, 3, bx * by, bz), bf16),
-            pltpu.VMEM((blocks * pairs, bz), bf16),
+            pltpu.VMEM((3, ndir * outer, bz), f32),
+            pltpu.VMEM((blocks * pairs, bz), f8),
             pltpu.VMEM((rows, 2 * blocks), bf16),
             pltpu.VMEM((3, rows, pairs), f32),
             pltpu.VMEM((rows, pairs), i32),
@@ -619,12 +639,9 @@
             dma((2, ndir)),
             dma((3, ndir)),
             dma((ndir,)),
-            dma((ndir,)),
-            dma((2, ndir)),
             dma,
             dma((2,)),
-            pltpu.SemaphoreType.REGULAR,
-            pltpu.SemaphoreType.REGULAR,
+            pltpu.SemaphoreType.REGULAR((2,)),
         ],
         compiler_params=pltpu.CompilerParams(collective_id=0, has_side_effects=True),
     )(live_blocks, pair_node, pair_line, pair_far, far_line, pair_geom, positions)

time: 48.3 us -> 47.3 us (0.979)
  Pallas kernels: 46.9 us -> 45.9 us
    pallas_call x1, Pallas kernels: 46 us -> 45 us  [local(): pl.pallas_call(functools.partial(kernel, sizes, blk), out_shape=(pltpu.VM...]
where the time goes in v3:
time: 47.3 us; the launch traced here: 47.2 us
  Pallas kernels  45.9 us (97%)
  between operations  1.29 us (3%)
    pallas_call x1, Pallas kernels, local(): pl.pallas_call(functools.partial(kernel, sizes, blk), out_shape=(pltpu.VM...  45 us

profile of v3, /device:TPU:1, one launch (start us, length us, event | category | flops | bytes accessed | tf_op | source)
XLA Modules:
  0.0 47.2 jit_solution(11976365840663716538)
XLA Ops:
  1.3 45.0 %shard_map.86 = (f32[3,16,16,256]{3,2,1,0:T(8,128)S(1)}, f32[2,5]{1,0:T(2,128)S(1)}) custom-call(s32[1,1,1]{2,1,0:T(1,128)S(6)} %copy.9.live_hbm, s32[1,1,1,32,256]{4,3,2,1,0:T(8,128)} %node_hbm.1, s32[1,1,1,32]{3,2,1,0:T(1,128)} %line_hbm.1, s32[1,1,1,32,256]{4,3,2,1,0:T(8,128)} %far_hbm.1, s32[1,1,1,32]{3,2,1,0:T(1,128)} %farline_hbm.1, ...), custom_call_target="tpu_custom_call" | custom-call | tf_op jit(solution)/shard_map/pallas_call | solution.py:600
  46.3 0.9 %shard_map.87 = (f32[3,16,16,256]{3,2,1,0:T(8,128)}, f32[2,5]{1,0:T(2,128)}) custom-call(f32[3,16,16,256]{3,2,1,0:T(8,128)S(1)} %get-tuple-element.4.moved, f32[2,5]{1,0:T(2,128)S(1)} %get-tuple-element.5.hist), custom_call_target="tpu_custom_call" | custom-call | tf_op jit(solution)/shard_map/pallas_call | solution.py:648
